TPU v7x, 32 devices: a whole 2x2x4 slice. The times are simulated.
32 devices in a mesh: arcs: 8 (over y, x, core), tiles: 4 (over z).
Axes of the slice: x: 2, y: 2, z: 4, core: 2. Of those that a mesh axis runs over, the one named last changes fastest.
Arguments:
- design: bfloat16 [12288, 8192], P('arcs', 'tiles'), may hold values from -0.09375 to 0.09375
- observations: float32 [12288], P('arcs'), may hold values from -25 to 25
- solution: float32 [8192], P('tiles'), may hold values from -6 to 6
- arc_ids: int32 [8, 1536], P('arcs'), may hold values from 0 to 3, never falling along the last dimension, each value on 1 to 768 neighbouring positions
- block_live: int32 [8, 12], P('arcs'), may hold values 0 or 1
Outputs:
- normal: float32 [8192, 8192], P('arcs', 'tiles')
- rhs: float32 [8192], P('tiles')
Inputs may be any that keep to these rules, and one draw needn't show every extreme that they name: `arc_ids`: the arcs of a group's rows never fall along its rows; an arc holds at most 768 rows and some arc exactly that many.
All inputs are finite; a program needn't handle non-finite values. No bound on the sum of `block_live` on one device may be relied on, other than what follows from the above.
Results may differ from a plain program's by a relative error of at most 0.0018.
Values may be sent and summed in bfloat16 or wider, within the bound.
A program may use at most 192 MiB of HBM per device.

v0:
```python
import jax
import jax.numpy as jnp
from jax import lax
from jax.sharding import PartitionSpec as P

ARCS_DEV = 4
prior_rows = 4.0


def contract_rows(left, right):
    return lax.dot_general(
        left, right, (((0,), (0,)), ((), ())), preferred_element_type=jnp.float32
    )


def local(design, observations, solution, arc_ids, block_live):
    row_count = design.shape[0]
    design_all = lax.all_gather(design, "tiles", axis=1, tiled=True)
    partial_value = jnp.dot(design.astype(jnp.float32), solution, precision=lax.Precision.HIGHEST)
    predicted = lax.psum(partial_value, "tiles")
    residual = observations - predicted
    live_row = (
        jnp.broadcast_to(block_live[0][:, None], (block_live.shape[1], 128))
        .reshape(row_count)
        .astype(jnp.float32)
    )
    arc_match = (arc_ids[0][None, :] == jnp.arange(ARCS_DEV, dtype=jnp.int32)[:, None]).astype(
        jnp.float32
    )
    squares = live_row * residual * residual
    arc_squares = jnp.sum(arc_match * squares[None, :], axis=1)
    arc_counts = jnp.sum(arc_match * live_row[None, :], axis=1)
    totals = lax.psum((jnp.sum(arc_squares), jnp.sum(arc_counts)), "arcs")
    variance_all = (totals[0] + 1.0) / (totals[1] + 1.0)
    arc_weight = variance_all / (
        (arc_squares + prior_rows * variance_all) / (arc_counts + prior_rows)
    )
    row_weight = live_row * jnp.sum(arc_match * arc_weight[:, None], axis=0)
    rhs_part = lax.dot_general(
        design.astype(jnp.float32),
        row_weight * residual,
        (((0,), (0,)), ((), ())),
        precision=lax.Precision.HIGHEST,
    )
    weighted = (row_weight[:, None] * design).astype(jnp.bfloat16)
    normal = lax.psum_scatter(
        contract_rows(design_all, weighted), "arcs", scatter_dimension=0, tiled=True
    )
    rhs = lax.psum(rhs_part, "arcs")
    return (normal, rhs)


def solution(mesh):
    return jax.shard_map(
        local,
        mesh=mesh,
        in_specs=(P("arcs", "tiles"), P("arcs"), P("tiles"), P("arcs", None), P("arcs", None)),
        out_specs=(P("arcs", "tiles"), P("tiles")),
        check_vma=False,
    )
```

profile of v0, /device:TPU:0, one launch (start us, length us, event | category | flops | bytes accessed | tf_op | source)
XLA Modules:
  0.0 898.4 jit_solution(16531943414175356195)
XLA Ops:
  7.2 0.0 copy-start
  7.2 0.0 copy-start.2
  7.2 0.0 copy-start.1
  7.2 0.0 all-gather.2.cloned.1.call-start
  7.2 0.7 all-gather.2.cloned.1.call-update
  7.9 0.0 reduce-scatter.2.cloned.1.call-start
  8.0 0.7 reduce.2
  8.7 0.0 copy-done
  8.7 7.0 convolution_reduce_fusion
  15.7 13.7 %psum.28 = f32[1536]{0:T(1024)S(1)} all-reduce(f32[1536]{0:T(1024)S(1)} %convolution_reduce_fusion), channel_id=1, replica_groups=mesh['arcs'=8,'tiles'=4] {'tiles'}, use_global_device_ids=true, to_apply=%region_0.0 | all-reduce | flops 1536 | bytes 12288 | tf_op jit(solution)/shard_map/psum | solution.py:20
  29.5 0.0 copy-done.2
  29.5 0.1 broadcast_bitcast_fusion
  29.6 0.0 copy-done.1
  29.6 0.1 multiply_multiply_fusion
  29.6 0.6 select_reduce_fusion.1
  30.3 13.2 %all-reduce = (f32[]{:T(128)}, f32[]{:T(128)}) all-reduce(f32[]{:T(128)} %get-tuple-element.11, f32[]{:T(128)} %get-tuple-element.6), channel_id=1, replica_groups=mesh['arcs'=8,'tiles'=4] {'arcs'}, use_global_device_ids=true, to_apply=%region_2.0 | all-reduce | flops 2 | bytes 16 | tf_op jit(solution)/shard_map/psum | solution.py:33
  44.9 0.1 select_reduce_fusion.4
  45.0 0.1 fusion.1
  45.0 392.5 %all-gather.2.cloned.1.call-done = bf16[1536,8192]{1,0:T(8,128)(2,1)} async-done(((bf16[1536,2048]{1,0:T(8,128)(2,1)}), bf16[1536,8192]{1,0:T(8,128)(2,1)}) %all-gather.2.cloned.1.call-update) | async-done | bytes 25165840 | tf_op jit(solution)/shard_map/all_gather | solution.py:18
  437.5 62.7 %convolution_bitcast_fusion = f32[8192,2048]{0,1:T(8,128)} fusion(bf16[1536,8192]{1,0:T(8,128)(2,1)} %all-gather.2.cloned.1.call-done, bf16[1536,2048]{1,0:T(8,128)(2,1)} %param.5, f32[1536]{0:T(1024)S(1)} %get-tuple-element.15), kind=kOutput, calls=%fused_computation | convolution fusion | flops 51549044736 | bytes 98572288 | tf_op jit(solution)/shard_map/dot_general | solution.py:11
  500.2 0.0 reduce-scatter.2.cloned.1.call-update
  500.3 4.6 fusion.2
  504.8 14.6 %psum.31 = f32[2048]{0:T(1024)} all-reduce(f32[2048]{0:T(1024)S(1)} %bitcast.19), channel_id=1, replica_groups=mesh['arcs'=8,'tiles'=4] {'arcs'}, use_global_device_ids=true, to_apply=%region_9.0 | all-reduce | flops 2048 | bytes 16384 | tf_op jit(solution)/shard_map/psum | solution.py:49
  519.5 363.0 %reduce-scatter.2.cloned.1.call-done = f32[1024,2048]{0,1:T(8,128)} async-done(((f32[8192,2048]{0,1:T(8,128)}), f32[1024,2048]{0,1:T(8,128)}) %reduce-scatter.2.cloned.1.call-update) | async-done | bytes 8388624 | tf_op jit(solution)/shard_map/reduce_scatter | solution.py:46
  882.4 9.1 %copy.8 = f32[1024,2048]{1,0:T(8,128)} copy(f32[1024,2048]{0,1:T(8,128)} %reduce-scatter.2.cloned.1.call-done) | data formatting | bytes 16777216
  (3 shorter events, 0.0 us)
Async XLA Ops:
  7.2 1.5 copy-start
  7.2 22.3 %copy-start.2 = (s32[1,12]{1,0:T(1,128)S(1)}, s32[1,12]{1,0:T(1,128)}, u32[]{:S(2)}) copy-start(s32[1,12]{1,0:T(1,128)} %param.9) | copy-start | bytes 148
  7.2 22.4 %copy-start.1 = (f32[1536]{0:T(1024)S(1)}, f32[1536]{0:T(1024)}, u32[]{:S(2)}) copy-start(f32[1536]{0:T(1024)} %param.6) | copy-start | bytes 18436
  7.2 430.3 %all-gather.2.cloned.1.call-start = ((), (), s32[]{:S(2)}) async-start(), calls=%async_computation.1 | async-start | bytes 31457280 | tf_op jit(solution)/shard_map/all_gather | solution.py:18
  7.9 874.5 %reduce-scatter.2.cloned.1.call-start = ((), (), s32[]{:S(2)}) async-start(), calls=%async_computation.2 | async-start | bytes 75497472 | tf_op jit(solution)/shard_map/reduce_scatter | solution.py:46
Sparse Core Ops, SparseCore 0:
  9.6 427.8 all-gather.1
  500.4 381.9 reduce-scatter.1
where the time goes:
time: 899 us; the launch traced here: 898 us
  waiting for transfers between devices  756 us (84%)
  matrix products  74.3 us (8%)
  blocking collectives  41.6 us (5%)
  between operations  15.5 us (2%)
  local copies, waits for them, and re-layouts  9.22 us (1%)
    all_gather x1, waiting for transfers between devices, local(): design_all = lax.all_gather(design, 'tiles', axis=1, tiled=True)  392 us
    reduce_scatter x1, waiting for transfers between devices, local(): lax.psum_scatter(contract_rows(design_all, weighted), 'arcs', scatter_dim...  363 us
    dot_general x1, matrix products, contract_rows(): lax.dot_general(left, right, (((0,), (0,)), ((), ())), preferred_element_...  62.7 us
  transfers between devices with their start and end apart: 2, of which 2 were waited for; matrix products, arithmetic and copies ran while one was open for 1% of the time, Pallas kernels for 0%

commit v1 on v0

--- a/solution.py
+++ b/solution.py
@@ -15,7 +15,9 @@
 
 def local(design, observations, solution, arc_ids, block_live):
     row_count = design.shape[0]
-    design_all = lax.all_gather(design, "tiles", axis=1, tiled=True)
+    design_all = jnp.concatenate(
+        lax.all_to_all(jnp.stack([design] * lax.axis_size("tiles")), "tiles", 0, 0), axis=1
+    )
     partial_value = jnp.dot(design.astype(jnp.float32), solution, precision=lax.Precision.HIGHEST)
     predicted = lax.psum(partial_value, "tiles")
     residual = observations - predicted

time: 899 us -> 1060 us (1.18)
  blocking collectives: 41.6 us -> 433 us
  waiting for transfers between devices: 756 us -> 497 us
  local copies, waits for them, and re-layouts: 9.22 us -> 28.6 us
    all_gather x1 -> x0, waiting for transfers between devices: 392 us -> none  [local(): design_all = lax.all_gather(design, 'tiles', axis=1, tiled=True)]
    psum x1, blocking collectives: 13.7 us -> 405 us  [local(): predicted = lax.psum(partial_value, 'tiles')]
    all_to_all x0 -> x1, waiting for transfers between devices: none -> 116 us  [local(): lax.all_to_all(jnp.stack([design] * lax.axis_size('tiles')), 'tiles', 0, 0)]
    reduce_scatter x1, waiting for transfers between devices: 363 us -> 381 us  [local(): lax.psum_scatter(contract_rows(design_all, weighted), 'arcs', scatter_dim...]
    another operation x0 -> x1, local copies, waits for them, and re-layouts: none -> 10.7 us  [local(): jnp.stack([design] * lax.axis_size('tiles'))]
where the time goes in v1:
time: 1060 us
  waiting for transfers between devices  497 us (47%)
  blocking collectives  433 us (41%)
  matrix products  75.8 us (7%)
  local copies, waits for them, and re-layouts  28.6 us (3%)
  between operations  15.5 us (1%)
    psum x1, blocking collectives, local(): predicted = lax.psum(partial_value, 'tiles')  405 us
    reduce_scatter x1, waiting for transfers between devices, local(): lax.psum_scatter(contract_rows(design_all, weighted), 'arcs', scatter_dim...  381 us
    all_to_all x1, waiting for transfers between devices, local(): lax.all_to_all(jnp.stack([design] * lax.axis_size('tiles')), 'tiles', 0, 0)  116 us
    dot_general x1, matrix products, contract_rows(): lax.dot_general(left, right, (((0,), (0,)), ((), ())), preferred_element_...  64.3 us
  transfers between devices with their start and end apart: 2, of which 2 were waited for; matrix products, arithmetic and copies ran while one was open for 1% of the time, Pallas kernels for 0%

profile of v1, /device:TPU:0, one launch (start us, length us, event | category | flops | bytes accessed | tf_op | source)
XLA Modules:
  0.0 1059.4 jit_solution(6140893146219128108)
XLA Ops:
  7.2 0.0 copy-start
  7.2 8.6 copy.10
  15.8 10.7 %stack.2 = bf16[4,1536,2048]{1,2,0:T(8,128)(2,1)} broadcast(bf16[1536,2048]{0,1:T(8,128)(2,1)} %copy.10), dimensions={1,2} | broadcast | bytes 31457280 | tf_op jit(solution)/shard_map/stack | solution.py:19
  26.5 0.0 copy-start.3
  26.5 8.6 all-to-all-start
  35.1 0.0 copy-start.4
  35.1 0.0 copy-start.2
  35.1 0.0 reduce-scatter.2.cloned.1.call-start
  35.2 0.0 copy-done.3
  35.2 0.0 copy-done
  35.2 7.0 convolution_reduce_fusion
  42.2 404.9 %psum.28 = f32[1536]{0:T(1024)S(1)} all-reduce(f32[1536]{0:T(1024)S(1)} %convolution_reduce_fusion), channel_id=1, replica_groups=mesh['arcs'=8,'tiles'=4] {'tiles'}, use_global_device_ids=true, to_apply=%region_0.0 | all-reduce | flops 1536 | bytes 12288 | tf_op jit(solution)/shard_map/psum | solution.py:22
  447.1 0.0 copy-done.4
  447.2 0.1 broadcast_bitcast_fusion
  447.2 0.0 copy-done.2
  447.2 0.1 multiply_multiply_fusion
  447.3 0.6 select_reduce_fusion.1
  447.9 14.1 %all-reduce = (f32[]{:T(128)}, f32[]{:T(128)}) all-reduce(f32[]{:T(128)} %get-tuple-element.13, f32[]{:T(128)} %get-tuple-element.8), channel_id=1, replica_groups=mesh['arcs'=8,'tiles'=4] {'arcs'}, use_global_device_ids=true, to_apply=%region_2.0 | all-reduce | flops 2 | bytes 16 | tf_op jit(solution)/shard_map/psum | solution.py:35
  463.4 0.1 select_reduce_fusion.4
  463.5 0.1 fusion.1
  463.5 116.4 %all-to-all-done = bf16[4,1536,2048]{1,2,0:T(8,128)(2,1)} async-done(((bf16[4,1536,2048]{1,2,0:T(8,128)(2,1)}), bf16[4,1536,2048]{1,2,0:T(8,128)(2,1)}, u32[]{:S(2)}, u32[]{:S(2)}) %all-to-all-start) | async-done | bytes 25165856 | tf_op jit(solution)/shard_map/all_to_all | solution.py:19
  579.9 64.3 %convolution_bitcast_fusion = f32[8192,2048]{0,1:T(8,128)} fusion(bf16[1536,8192]{0,1:T(8,128)(2,1)} %bitcast.4, bf16[1536,2048]{1,0:T(8,128)(2,1)} %param.5, f32[1536]{0:T(1024)S(1)} %get-tuple-element.17), kind=kOutput, calls=%fused_computation | convolution fusion | flops 51549044736 | bytes 98572288 | tf_op jit(solution)/shard_map/dot_general | solution.py:11
  644.2 0.0 reduce-scatter.2.cloned.1.call-update
  644.2 4.6 fusion.2
  648.8 0.0 copy-start.1
  648.8 13.7 %psum.31 = f32[2048]{0:T(1024)} all-reduce(f32[2048]{0:T(1024)S(1)} %bitcast.22), channel_id=1, replica_groups=mesh['arcs'=8,'tiles'=4] {'arcs'}, use_global_device_ids=true, to_apply=%region_9.0 | all-reduce | flops 2048 | bytes 16384 | tf_op jit(solution)/shard_map/psum | solution.py:51
  662.5 380.9 %reduce-scatter.2.cloned.1.call-done = f32[1024,2048]{0,1:T(8,128)} async-done(((f32[8192,2048]{0,1:T(8,128)}), f32[1024,2048]{0,1:T(8,128)}) %reduce-scatter.2.cloned.1.call-update) | async-done | bytes 8388624 | tf_op jit(solution)/shard_map/reduce_scatter | solution.py:48
  1043.4 9.1 copy.11
  1052.5 0.0 copy-done.1
  (4 shorter events, 0.0 us)
Async XLA Ops:
  7.2 28.1 %copy-start = (f32[2048]{0:T(1024)S(1)}, f32[2048]{0:T(1024)}, u32[]{:S(2)}) copy-start(f32[2048]{0:T(1024)} %param.7) | copy-start | bytes 24580
  26.5 8.7 copy-start.3
  26.5 553.4 %all-to-all-start = ((bf16[4,1536,2048]{1,2,0:T(8,128)(2,1)}), bf16[4,1536,2048]{1,2,0:T(8,128)(2,1)}, u32[]{:S(2)}, u32[]{:S(2)}) async-start(bf16[4,1536,2048]{1,2,0:T(8,128)(2,1)} %stack.2), calls=%async_computation | async-start | bytes 50331648 | tf_op jit(solution)/shard_map/all_to_all | solution.py:19
  35.1 412.0 %copy-start.4 = (s32[1,12]{1,0:T(1,128)S(1)}, s32[1,12]{1,0:T(1,128)}, u32[]{:S(2)}) copy-start(s32[1,12]{1,0:T(1,128)} %param.9) | copy-start | bytes 148
  35.1 412.1 %copy-start.2 = (f32[1536]{0:T(1024)S(1)}, f32[1536]{0:T(1024)}, u32[]{:S(2)}) copy-start(f32[1536]{0:T(1024)} %param.6) | copy-start | bytes 18436
  35.1 1008.3 %reduce-scatter.2.cloned.1.call-start = ((), (), s32[]{:S(2)}) async-start(), calls=%async_computation.2 | async-start | bytes 75497472 | tf_op jit(solution)/shard_map/reduce_scatter | solution.py:48
  648.8 403.7 %copy-start.1 = (f32[2048]{0:T(1024)S(1)}, f32[2048]{0:T(1024)}, u32[]{:S(2)}) copy-start(f32[2048]{0:T(1024)} %param.7) | copy-start | bytes 24580
Sparse Core Ops, SparseCore 0:
  644.3 399.0 reduce-scatter.1
